TPU v7x, 32 devices: a whole 2x2x4 slice. The times are simulated.
32 devices in a mesh: cls: 4 (over z), site: 8 (over y, x, core).
Axes of the slice: x: 2, y: 2, z: 4, core: 2. Of those that a mesh axis runs over, the one named last changes fastest.
Arguments:
- tip_codes: int32 [1024, 8192], P('cls', 'site'), may hold values from 0 to 3
- counts: int32 [8192], P('site'), may hold values from 1 to 5
- children: int32 [1023, 2], replicated, may hold values from 0 to 2045, as said below
- lengths: float32 [4, 2046], replicated, may hold values from 0.01 to 1
- frequencies: float32 [4, 4], replicated, may hold values from 0.25 to 1.75
- weights: float32 [4], replicated, may hold values from 0.2 to 1
Outputs:
- site_loglik: float32 [4, 2048], P('cls', 'site')
- new_weights: float32 [4], P('cls')
- mean_loglik: float32 [], replicated
Inputs may be any that keep to these rules, and one draw needn't show every extreme that they name: Row k lists the two children of internal node 1024 + k as node ids. Give the tips height 0 and the root height 10. The nodes of height h + 1 have exactly the nodes of height h as children, each once, and the root is node 2046. For every height h from 0 to 5, split the parents (height h + 1) and the children (height h) into 16 equal aligned blocks: the children of parent block j are child block j, so the tips j * 64 onward form clade j.
All inputs are finite; a program needn't handle non-finite values.
Results may differ from a plain program's by a relative error of at most 0.0003.
Values sent between devices are 32-bit elements; how exact they have to be, the bound alone decides.
A program may use at most 64 MiB of HBM per device.

v0:
```python
import functools

import jax
import jax.numpy as jnp
from jax import lax
from jax.experimental import pallas as pl
from jax.experimental.pallas import tpu as pltpu
from jax.sharding import PartitionSpec as P

LEVELS = 10
TOP = 4
LANES = 128
MESH = pl.DeviceIdType.MESH


def level_base(taxa, h):
    return 0 if h == 0 else 2 * taxa - (taxa >> (h - 1))


def kernel(
    groups,
    site_devices,
    codes_hbm,
    counts_ref,
    kids_ref,
    kids_smem,
    lengths_ref,
    freq_ref,
    weights_ref,
    result,
    codes,
    picked,
    table,
    grow,
    grow_up,
    stat,
    sent,
    got,
    upper,
    part,
    part_got,
    group_sum,
    group_got,
    code_sem,
    send_sem,
    recv_sem,
    part_send,
    part_recv,
    sum_send,
    sum_recv,
):
    g = lax.axis_index("cls")
    me = lax.axis_index("site")
    local, sites = codes_hbm.shape
    taxa = local * groups
    classes, branches = lengths_ref.shape
    quarter = sites // groups
    halves = quarter // LANES
    low = LEVELS - TOP
    clades = local >> low
    rows = halves * classes
    f32 = jnp.float32
    bf16 = jnp.bfloat16

    fetch = pltpu.make_async_copy(codes_hbm, codes, code_sem)
    fetch.start()

    barrier = pltpu.get_barrier_semaphore()
    for k in range(1, groups):
        pl.semaphore_signal(
            barrier, inc=1, device_id={"cls": lax.rem(g + k, groups)}, device_id_type=MESH
        )
    for k in range(1, site_devices):
        pl.semaphore_signal(
            barrier,
            inc=1,
            device_id={"site": lax.rem(me + k, site_devices)},
            device_id_type=MESH,
        )

    freq = freq_ref[...]
    pi = freq / jnp.sum(freq, axis=1, keepdims=True)
    beta = 1.0 / (1.0 - jnp.sum(pi * pi, axis=1, keepdims=True))
    lengths = lengths_ref[...]
    r = jnp.exp(beta * lengths) - 1.0
    drift = beta * jnp.sum(lengths, axis=1, keepdims=True)

    table[...] = jnp.zeros_like(table)
    hi = r.astype(bf16).astype(f32)
    rest = r - hi
    mid = rest.astype(bf16).astype(f32)
    table[0:classes, 0:branches] = hi
    table[classes : 2 * classes, 0:branches] = mid
    table[2 * classes : 3 * classes, 0:branches] = rest - mid
    kids = kids_ref[...]
    table[12:14, taxa : taxa + kids.shape[1]] = (kids >> 8).astype(f32)
    table[14:16, taxa : taxa + kids.shape[1]] = (kids & 255).astype(f32)

    pi8 = jnp.concatenate([pi] * halves, axis=0)
    for c in range(classes):
        for i in range(4):
            wide = jnp.broadcast_to(pi[:, i : i + 1], (classes, LANES))
            stat[c, i] = jnp.broadcast_to(wide[c : c + 1], (8, LANES))
    first_up = level_base(taxa, low)
    window = first_up // LANES * LANES
    r8 = jnp.concatenate([r[:, window:branches]] * halves, axis=0)
    for j in range(branches - first_up):
        at = first_up - window + j
        grow_up[j] = jnp.broadcast_to(r8[:, at : at + 1], (rows, LANES))

    q = lax.broadcasted_iota(jnp.int32, (1, local), 1)
    ancestor = (first_up + g * clades + (q & (clades - 1))).astype(f32)
    offset = {}
    total_rows = 0
    for h in range(low):
        offset[h] = total_rows
        total_rows += local >> h
    for h in range(low, -1, -1):
        count = local >> h
        base = level_base(taxa, h)
        if count % LANES == 0:
            start = pl.multiple_of(base + g * count, LANES)
            width = count
        else:
            start = base // LANES * LANES
            end = base + (taxa >> h)
            width = -(-end // LANES) * LANES - start
        ids = lax.broadcasted_iota(jnp.int32, (width, local), 0) + start
        onehot = (ids.astype(f32) == ancestor).astype(f32).astype(bf16)
        part_table = table[:, pl.ds(start, width)].astype(bf16)
        out = jnp.dot(part_table, onehot, preferred_element_type=f32)
        if h < low:
            r_row = out[0:classes] + out[classes : 2 * classes] + out[2 * classes : 3 * classes]
            r_col = jnp.concatenate([r_row, r_row], axis=0).T
            for c in range(classes):
                grow[c, offset[h] : offset[h] + count, :] = jnp.broadcast_to(
                    r_col[:count, c : c + 1], (count, LANES)
                )
        if h > 0:
            left = out[12:13] * 256.0 + out[14:15]
            right = out[13:14] * 256.0 + out[15:16]
            ancestor = jnp.where((q & count) != 0, right, left)
    tip_col = jnp.broadcast_to(ancestor, (8, local)).T[:, 0:1]
    tip_ids = (lax.broadcasted_iota(jnp.int32, (local, local), 1) + g * local).astype(f32)
    order = (tip_ids == tip_col).astype(f32).astype(bf16)

    fetch.wait()

    def quarter_of(k, dest):
        block = lax.rem(g + k, groups)
        for half in range(halves):
            lanes = pl.ds(pl.multiple_of(block * quarter + half * LANES, LANES), LANES)
            picked[half] = jnp.dot(
                order, codes[:, lanes].astype(f32).astype(bf16), preferred_element_type=f32
            )

        def one(step, carry):
            half = step // (classes // 2)
            pair = lax.rem(step, classes // 2) * 2
            both = (0, 1)
            pis = [[stat[pair + b, i] for i in range(4)] for b in both]

            def factor(b, h, n):
                return grow[pair + b, offset[h] + 8 * n : offset[h] + 8 * n + 8, :]

            def tip(n):
                code = picked[half, 8 * n : 8 * n + 8, :]
                marks = [code == float(i) for i in range(4)]
                result = []
                for b in both:
                    own = jnp.where(marks[2], pis[b][2], pis[b][3])
                    own = jnp.where(marks[0], pis[b][0], jnp.where(marks[1], pis[b][1], own))
                    off = factor(b, 0, n) * own
                    on = off + 1.0
                    result.append([jnp.where(mark, on, off) for mark in marks])
                return result

            def spread(b, values, scale):
                mean = (values[0] * pis[b][0] + values[1] * pis[b][1]) + (
                    values[2] * pis[b][2] + values[3] * pis[b][3]
                )
                move = scale * mean
                return [value + move for value in values]

            logs = ([], [])

            def node(h, n):
                if h == 0:
                    return tip(n)
                gap = (local >> h) // 8
                left = node(h - 1, n)
                right = node(h - 1, n + gap)
                result = []
                for b in both:
                    one_left, one_right = left[b], right[b]
                    if h > 1:
                        one_left = spread(b, one_left, factor(b, h - 1, n))
                        one_right = spread(b, one_right, factor(b, h - 1, n + gap))
                    values = [x * y for x, y in zip(one_left, one_right)]
                    if h == 3:
                        largest = jnp.maximum(
                            jnp.maximum(values[0], values[1]), jnp.maximum(values[2], values[3])
                        )
                        scale = pl.reciprocal(largest, approx=True)
                        logs[b].append(jnp.log(scale))
                        values = [value * scale for value in values]
                    result.append(values)
                return result

            ends = node(low - 1, 0)
            for b in both:
                row = pl.ds(half * classes + pair + b, 1)
                values = spread(b, ends[b], factor(b, low - 1, 0))
                values = [value[0:clades] * value[clades : 2 * clades] for value in values]
                log_sum = jnp.sum(sum(logs[b][1:], logs[b][0]), axis=0, keepdims=True)
                log_sum = jnp.sum(jnp.log(values[3]), axis=0, keepdims=True) - log_sum
                inverse = 1.0 / values[3]
                for i in range(3):
                    ratio = values[i] * inverse
                    for j in range(clades):
                        dest[j * 3 + i, row, :] = ratio[j : j + 1]
                dest[clades * 3, row, :] = log_sum
            return carry

        lax.fori_loop(0, rows // 2, one, 0)

    copies = []
    for place, k in enumerate([2, 1, 3] if groups == 4 else range(1, groups)):
        quarter_of(k, sent.at[k])
        if place == 0:
            pl.semaphore_wait(barrier, groups + site_devices - 2)
        copy = pltpu.make_async_remote_copy(
            src_ref=sent.at[k],
            dst_ref=got.at[k],
            send_sem=send_sem.at[k],
            recv_sem=recv_sem.at[k],
            device_id={"cls": lax.rem(g + k, groups)},
            device_id_type=MESH,
        )
        copy.start()
        copies.append(copy)
    quarter_of(0, got.at[0])
    for copy in copies:
        copy.wait()

    pis8 = [jnp.broadcast_to(pi8[:, i : i + 1], (rows, LANES)) for i in range(4)]
    scales = got[0, clades * 3]
    for k in range(1, groups):
        scales = scales + got[k, clades * 3]

    def child(tree_level, ident):
        if tree_level == low:
            clade = jnp.clip(ident - first_up, 0, 2**TOP - 1)
            k = lax.rem(g + groups - clade // clades, groups)
            row = lax.rem(clade, clades) * 3
            values = [got[k, row + i] for i in range(3)] + [jnp.ones((rows, LANES), f32)]
        else:
            at = jnp.clip(ident - level_base(taxa, low + 1), 0, 2**TOP - 1)
            values = [upper[at, i] for i in range(4)]
        mean = (values[0] * pis8[0] + values[1] * pis8[1]) + (
            values[2] * pis8[2] + values[3] * pis8[3]
        )
        move = grow_up[jnp.clip(ident - first_up, 0, branches - first_up - 1)] * mean
        return [value + move for value in values]

    place = 0
    for tree_level in range(low, LEVELS):
        count = taxa >> (tree_level + 1)
        first = taxa - (taxa >> tree_level)
        for n in range(count):
            left = child(tree_level, kids_smem[0, first + n])
            right = child(tree_level, kids_smem[1, first + n])
            values = [a * b for a, b in zip(left, right)]
            largest = jnp.maximum(
                jnp.maximum(values[0], values[1]), jnp.maximum(values[2], values[3])
            )
            scale = pl.reciprocal(largest, approx=True)
            scales = scales - jnp.log(scale)
            values = [value * scale for value in values]
            if tree_level < LEVELS - 1:
                for i in range(4):
                    upper[place, i] = values[i]
                place += 1
    end = (values[0] * pis8[0] + values[1] * pis8[1]) + (
        values[2] * pis8[2] + values[3] * pis8[3]
    )
    spot = lax.broadcasted_iota(jnp.int32, (classes, classes), 0)
    spot = spot == lax.broadcasted_iota(jnp.int32, (classes, classes), 1)
    weights = jnp.sum(jnp.where(spot, weights_ref[...], 0.0), axis=1, keepdims=True)
    log_weight = jnp.log(weights / jnp.sum(weights, axis=0, keepdims=True))
    bias = jnp.concatenate([log_weight - drift] * halves, axis=0)
    shifted = scales + jnp.log(end) + bias

    mass = jnp.zeros((classes, LANES), f32)
    loglik = jnp.zeros((1, LANES), f32)
    seen = jnp.zeros((1, LANES), f32)
    for half in range(halves):
        a = shifted[half * classes : (half + 1) * classes]
        top = jnp.max(a, axis=0, keepdims=True)
        total = top + jnp.log(jnp.sum(jnp.exp(a - top), axis=0, keepdims=True))
        n = counts_ref[pl.ds(g * halves + half, 1), :].astype(f32)
        result[half : half + 1, :] = total / taxa
        mass = mass + n * jnp.exp(a - total)
        loglik = loglik + n * total
        seen = seen + n
    part[...] = jnp.zeros_like(part)
    part[0:classes] = mass
    part[classes : classes + 1] = loglik
    part[classes + 1 : classes + 2] = seen

    copies = []
    for k in range(1, groups):
        copy = pltpu.make_async_remote_copy(
            src_ref=part,
            dst_ref=part_got.at[k],
            send_sem=part_send.at[k],
            recv_sem=part_recv.at[k],
            device_id={"cls": lax.rem(g + k, groups)},
            device_id_type=MESH,
        )
        copy.start()
        copies.append(copy)
    for copy in copies:
        copy.wait()
    part_got[0] = part[...]
    sums = part_got[lax.rem(g + groups, groups)]
    for d in range(1, groups):
        sums = sums + part_got[lax.rem(g + groups - d, groups)]
    group_sum[...] = sums
    copies = []
    for k in range(1, site_devices):
        copy = pltpu.make_async_remote_copy(
            src_ref=group_sum,
            dst_ref=group_got.at[k],
            send_sem=sum_send.at[k],
            recv_sem=sum_recv.at[k],
            device_id={"site": lax.rem(me + k, site_devices)},
            device_id_type=MESH,
        )
        copy.start()
        copies.append(copy)
    for copy in copies:
        copy.wait()
    group_got[0] = sums
    sums = group_got[lax.rem(me + site_devices, site_devices)]
    for d in range(1, site_devices):
        sums = sums + group_got[lax.rem(me + site_devices - d, site_devices)]
    line = jnp.sum(sums, axis=1, keepdims=True)
    all_count = line[classes + 1 : classes + 2]
    mean = line[classes : classes + 1] / (all_count * taxa)
    share = line[0:classes] / all_count
    mine = lax.broadcasted_iota(jnp.int32, (classes, 1), 0) == g
    share = jnp.sum(jnp.where(mine, share, 0.0), axis=0, keepdims=True)
    result[halves : halves + 1, :] = jnp.broadcast_to(share, (1, LANES))
    result[halves + 1 : halves + 2, :] = jnp.broadcast_to(mean, (1, LANES))


def finish(result, site_out, weight_out, mean_out):
    halves = result.shape[0] - 2
    for half in range(halves):
        site_out[0:1, half * LANES : (half + 1) * LANES] = result[half : half + 1, :]
    weight_out[...] = result[halves : halves + 1, 0:1]
    mean_out[...] = result[halves + 1 : halves + 2, 0:1]


def solution(mesh):
    groups = mesh.shape["cls"]
    site_devices = mesh.shape["site"]

    def per_device(tip_codes, counts, children, lengths, frequencies, weights):
        local, sites = tip_codes.shape
        taxa = local * groups
        classes, branches = lengths.shape
        quarter = sites // groups
        halves = quarter // LANES
        rows = halves * classes
        low = LEVELS - TOP
        clades = local >> low
        low_rows = sum(local >> h for h in range(low))
        table_width = -(-(branches + 1) // LANES) * LANES
        up_count = branches - level_base(taxa, low)
        kids = children.T
        vmem = pl.BlockSpec(memory_space=pltpu.VMEM)
        smem = pl.BlockSpec(memory_space=pltpu.SMEM)
        f32 = jnp.float32
        result = pl.pallas_call(
            functools.partial(kernel, groups, site_devices),
            out_shape=jax.ShapeDtypeStruct((halves + 2, LANES), f32),
            in_specs=[pl.BlockSpec(memory_space=pl.ANY), vmem, vmem, smem, vmem, vmem, vmem],
            out_specs=vmem,
            scratch_shapes=[
                pltpu.VMEM((local, sites), jnp.int32),
                pltpu.VMEM((halves, local, LANES), f32),
                pltpu.VMEM((16, table_width), f32),
                pltpu.VMEM((classes, low_rows, LANES), f32),
                pltpu.VMEM((up_count, rows, LANES), f32),
                pltpu.VMEM((classes, 4, 8, LANES), f32),
                pltpu.VMEM((groups, clades * 3 + 1, rows, LANES), f32),
                pltpu.VMEM((groups, clades * 3 + 1, rows, LANES), f32),
                pltpu.VMEM((2 ** TOP, 4, rows, LANES), f32),
                pltpu.VMEM((8, LANES), f32),
                pltpu.VMEM((groups, 8, LANES), f32),
                pltpu.VMEM((8, LANES), f32),
                pltpu.VMEM((site_devices, 8, LANES), f32),
                pltpu.SemaphoreType.DMA,
                pltpu.SemaphoreType.DMA((groups,)),
                pltpu.SemaphoreType.DMA((groups,)),
                pltpu.SemaphoreType.DMA((groups,)),
                pltpu.SemaphoreType.DMA((groups,)),
                pltpu.SemaphoreType.DMA((site_devices,)),
                pltpu.SemaphoreType.DMA((site_devices,)),
            ],
            compiler_params=pltpu.CompilerParams(collective_id=0, has_side_effects=True),
        )(
            tip_codes,
            counts.reshape(sites // LANES, LANES),
            kids,
            kids,
            lengths,
            frequencies,
            weights.reshape(1, classes),
        )
        site_loglik, new_weights, mean_loglik = pl.pallas_call(
            finish,
            out_shape=(
                jax.ShapeDtypeStruct((1, quarter), f32),
                jax.ShapeDtypeStruct((1, 1), f32),
                jax.ShapeDtypeStruct((1, 1), f32),
            ),
            in_specs=[vmem],
            out_specs=(vmem, vmem, vmem),
        )(result)
        return site_loglik, new_weights.reshape(1), mean_loglik.reshape(())

    return jax.shard_map(
        per_device,
        mesh=mesh,
        in_specs=(P("cls", "site"), P("site"), P(), P(), P(), P()),
        out_specs=(P("cls", "site"), P("cls"), P()),
        check_vma=False,
    )
```

profile of v0, /device:TPU:0, one launch (start us, length us, event | category | flops | bytes accessed | tf_op | source)
XLA Modules:
  0.0 23.9 jit_solution(7960195250028018550)
XLA Ops:
  0.6 22.1 %shard_map.85.result = f32[4,128]{1,0:T(4,128)} custom-call(s32[256,1024]{1,0:T(8,128)} %codes_hbm.1, s32[8,128]{1,0:T(8,128)} %bitcast.7, s32[2,1023]{1,0:T(2,128)} %bitcast.5, s32[2,1023]{1,0:T(2,128)} %bitcast.6, f32[4,2046]{1,0:T(4,128)} %lengths_ref.1, f32[4,4]{1,0:T(4,128)} %freq_ref.1, f32[1,4]{1,0:T(1,128)} %bitcast.8), custom_call_target="tpu_custom_call" | custom-call | tf_op jit(solution)/shard_map/pallas_call | solution.py:386
  22.7 1.2 %shard_map.86 = (f32[1,256]{1,0:T(1,128)}, f32[1,1]{1,0:T(1,128)}, f32[1,1]{1,0:T(1,128)}) custom-call(f32[4,128]{1,0:T(4,128)} %shard_map.85.result), custom_call_target="tpu_custom_call" | custom-call | tf_op jit(solution)/shard_map/pallas_call | solution.py:423
where the time goes:
time: 24.2 us; the launch traced here: 23.9 us
  Pallas kernels  23.3 us (96%)
  between operations  0.64 us (3%)
    pallas_call x1, Pallas kernels, per_device(): pl.pallas_call(functools.partial(kernel, groups, site_devices), out_shape...  22.1 us
    pallas_call x1, Pallas kernels, per_device(): pl.pallas_call(finish, out_shape=(jax.ShapeDtypeStruct((1, quarter), f32)...  1.24 us

commit v1 on v0

--- a/solution.py
+++ b/solution.py
@@ -39,15 +39,11 @@
     upper,
     part,
     part_got,
-    group_sum,
-    group_got,
     code_sem,
     send_sem,
     recv_sem,
     part_send,
     part_recv,
-    sum_send,
-    sum_recv,
 ):
     g = lax.axis_index("cls")
     me = lax.axis_index("site")
@@ -66,15 +62,12 @@
     fetch.start()
 
     barrier = pltpu.get_barrier_semaphore()
-    for k in range(1, groups):
-        pl.semaphore_signal(
-            barrier, inc=1, device_id={"cls": lax.rem(g + k, groups)}, device_id_type=MESH
-        )
-    for k in range(1, site_devices):
+    others = [(a, b) for a in range(groups) for b in range(site_devices) if a or b]
+    for a, b in others:
         pl.semaphore_signal(
             barrier,
             inc=1,
-            device_id={"site": lax.rem(me + k, site_devices)},
+            device_id={"cls": lax.rem(g + a, groups), "site": lax.rem(me + b, site_devices)},
             device_id_type=MESH,
         )
 
@@ -228,7 +221,7 @@
     for place, k in enumerate([2, 1, 3] if groups == 4 else range(1, groups)):
         quarter_of(k, sent.at[k])
         if place == 0:
-            pl.semaphore_wait(barrier, groups + site_devices - 2)
+            pl.semaphore_wait(barrier, len(others))
         copy = pltpu.make_async_remote_copy(
             src_ref=sent.at[k],
             dst_ref=got.at[k],
@@ -303,54 +296,33 @@
         mass = mass + n * jnp.exp(a - total)
         loglik = loglik + n * total
         seen = seen + n
-    part[...] = jnp.zeros_like(part)
-    part[0:classes] = mass
-    part[classes : classes + 1] = loglik
-    part[classes + 1 : classes + 2] = seen
-
-    copies = []
-    for k in range(1, groups):
-        copy = pltpu.make_async_remote_copy(
-            src_ref=part,
-            dst_ref=part_got.at[k],
-            send_sem=part_send.at[k],
-            recv_sem=part_recv.at[k],
-            device_id={"cls": lax.rem(g + k, groups)},
+    for c in range(classes):
+        part[c, 0:1] = mass[c : c + 1]
+        part[c, 1:2] = loglik
+        part[c, 2:3] = seen
+        part[c, 3:4] = jnp.zeros_like(seen)
+    own = g * site_devices + me
+    for a, b in reversed(others):
+        target = lax.rem(g + a, groups)
+        pltpu.make_async_remote_copy(
+            src_ref=part.at[target],
+            dst_ref=part_got.at[own],
+            send_sem=part_send,
+            recv_sem=part_recv,
+            device_id={"cls": target, "site": lax.rem(me + b, site_devices)},
             device_id_type=MESH,
-        )
-        copy.start()
-        copies.append(copy)
-    for copy in copies:
-        copy.wait()
-    part_got[0] = part[...]
-    sums = part_got[lax.rem(g + groups, groups)]
-    for d in range(1, groups):
-        sums = sums + part_got[lax.rem(g + groups - d, groups)]
-    group_sum[...] = sums
-    copies = []
-    for k in range(1, site_devices):
-        copy = pltpu.make_async_remote_copy(
-            src_ref=group_sum,
-            dst_ref=group_got.at[k],
-            send_sem=sum_send.at[k],
-            recv_sem=sum_recv.at[k],
-            device_id={"site": lax.rem(me + k, site_devices)},
-            device_id_type=MESH,
-        )
-        copy.start()
-        copies.append(copy)
-    for copy in copies:
-        copy.wait()
-    group_got[0] = sums
-    sums = group_got[lax.rem(me + site_devices, site_devices)]
-    for d in range(1, site_devices):
-        sums = sums + group_got[lax.rem(me + site_devices - d, site_devices)]
+        ).start()
+    part_got[own] = part[g]
+    arrivals = part_got.at[pl.ds(0, len(others))]
+    pltpu.make_async_copy(arrivals, arrivals, part_recv).wait()
+    sums = part_got[0]
+    for d in range(1, groups * site_devices):
+        sums = sums + part_got[d]
     line = jnp.sum(sums, axis=1, keepdims=True)
-    all_count = line[classes + 1 : classes + 2]
-    mean = line[classes : classes + 1] / (all_count * taxa)
-    share = line[0:classes] / all_count
-    mine = lax.broadcasted_iota(jnp.int32, (classes, 1), 0) == g
-    share = jnp.sum(jnp.where(mine, share, 0.0), axis=0, keepdims=True)
+    all_count = line[2:3]
+    mean = line[1:2] / (all_count * taxa)
+    share = line[0:1] / all_count
+    pltpu.make_async_copy(arrivals, arrivals, part_send).wait()
     result[halves : halves + 1, :] = jnp.broadcast_to(share, (1, LANES))
     result[halves + 1 : halves + 2, :] = jnp.broadcast_to(mean, (1, LANES))
 
@@ -398,17 +370,13 @@
                 pltpu.VMEM((groups, clades * 3 + 1, rows, LANES), f32),
                 pltpu.VMEM((groups, clades * 3 + 1, rows, LANES), f32),
                 pltpu.VMEM((2 ** TOP, 4, rows, LANES), f32),
-                pltpu.VMEM((8, LANES), f32),
-                pltpu.VMEM((groups, 8, LANES), f32),
-                pltpu.VMEM((8, LANES), f32),
-                pltpu.VMEM((site_devices, 8, LANES), f32),
+                pltpu.VMEM((classes, 4, LANES), f32),
+                pltpu.VMEM((groups * site_devices, 4, LANES), f32),
                 pltpu.SemaphoreType.DMA,
                 pltpu.SemaphoreType.DMA((groups,)),
                 pltpu.SemaphoreType.DMA((groups,)),
-                pltpu.SemaphoreType.DMA((groups,)),
-                pltpu.SemaphoreType.DMA((groups,)),
-                pltpu.SemaphoreType.DMA((site_devices,)),
-                pltpu.SemaphoreType.DMA((site_devices,)),
+                pltpu.SemaphoreType.DMA,
+                pltpu.SemaphoreType.DMA,
             ],
             compiler_params=pltpu.CompilerParams(collective_id=0, has_side_effects=True),
         )(

time: 24.2 us -> 22.4 us (0.926)
  Pallas kernels: 23.3 us -> 21.6 us
    pallas_call x1, Pallas kernels: 22.1 us -> 20.3 us  [per_device(): pl.pallas_call(functools.partial(kernel, groups, site_devices), out_shape...]
where the time goes in v1:
time: 22.4 us; the launch traced here: 22.2 us
  Pallas kernels  21.6 us (96%)
  between operations  0.64 us (3%)
    pallas_call x1, Pallas kernels, per_device(): pl.pallas_call(functools.partial(kernel, groups, site_devices), out_shape...  20.3 us
    pallas_call x1, Pallas kernels, per_device(): pl.pallas_call(finish, out_shape=(jax.ShapeDtypeStruct((1, quarter), f32)...  1.24 us

profile of v1, /device:TPU:0, one launch (start us, length us, event | category | flops | bytes accessed | tf_op | source)
XLA Modules:
  0.0 22.2 jit_solution(6474771808965835225)
XLA Ops:
  0.6 20.3 %shard_map.85.result = f32[4,128]{1,0:T(4,128)} custom-call(s32[256,1024]{1,0:T(8,128)} %codes_hbm.1, s32[8,128]{1,0:T(8,128)} %bitcast.7, s32[2,1023]{1,0:T(2,128)} %bitcast.5, s32[2,1023]{1,0:T(2,128)} %bitcast.6, f32[4,2046]{1,0:T(4,128)} %lengths_ref.1, f32[4,4]{1,0:T(4,128)} %freq_ref.1, f32[1,4]{1,0:T(1,128)} %bitcast.8), custom_call_target="tpu_custom_call" | custom-call | tf_op jit(solution)/shard_map/pallas_call | solution.py:358
  21.0 1.2 %shard_map.86 = (f32[1,256]{1,0:T(1,128)}, f32[1,1]{1,0:T(1,128)}, f32[1,1]{1,0:T(1,128)}) custom-call(f32[4,128]{1,0:T(4,128)} %shard_map.85.result), custom_call_target="tpu_custom_call" | custom-call | tf_op jit(solution)/shard_map/pallas_call | solution.py:391

commit v2 on v1

v2 whole, which is shorter than its diff:
```python
import functools

import jax
import jax.numpy as jnp
from jax import lax
from jax.experimental import pallas as pl
from jax.experimental.pallas import tpu as pltpu
from jax.sharding import PartitionSpec as P

LEVELS = 10
TOP = 4
LANES = 128
PIECES = 1
MESH = pl.DeviceIdType.MESH


def level_base(taxa, h):
    return 0 if h == 0 else 2 * taxa - (taxa >> (h - 1))


def look_up(table, index):
    numbers = lax.GatherDimensionNumbers(
        offset_dims=(),
        collapsed_slice_dims=(0,),
        start_index_map=(0,),
        operand_batching_dims=(1,),
        start_indices_batching_dims=(1,),
    )
    return lax.gather(
        table,
        index[..., None],
        numbers,
        (1, 1),
        mode=lax.GatherScatterMode.PROMISE_IN_BOUNDS,
    )


def kernel(
    groups,
    site_devices,
    codes_hbm,
    counts_hbm,
    kids_hbm,
    lengths_hbm,
    freq_hbm,
    weights_hbm,
    result,
    codes,
    counts,
    kids,
    lengths_ref,
    freq_ref,
    weights_ref,
    table,
    tail,
    grow,
    grow_up,
    stat,
    pick,
    pairs,
    mids,
    scale_sum,
    sent,
    got,
    sent_scale,
    got_scale,
    upper,
    part,
    part_got,
    in_sem,
    code_sem,
    send_sem,
    recv_sem,
    scale_send,
    scale_recv,
    part_send,
    part_recv,
):
    g = lax.axis_index("cls")
    me = lax.axis_index("site")
    tiles, folds, _, _ = codes.shape
    local = tiles * 8
    taxa = local * groups
    classes, branches = lengths_ref.shape
    halves = folds // groups
    low = LEVELS - TOP
    clades = local >> low
    rows = halves * classes
    f32 = jnp.float32

    copies = []
    small = [
        (freq_hbm, freq_ref),
        (lengths_hbm, lengths_ref),
        (kids_hbm, kids),
        (weights_hbm, weights_ref),
        (counts_hbm, counts),
    ]
    for n, (source, target) in enumerate(small):
        copies.append(pltpu.make_async_copy(source, target, in_sem.at[n]))
        copies[-1].start()
    fetches = []
    for fold in range(folds):
        lanes = pl.ds(fold * LANES, LANES)
        fetches.append(
            pltpu.make_async_copy(codes_hbm.at[:, :, lanes], codes.at[:, fold], code_sem.at[fold])
        )
        fetches[-1].start()

    barrier = pltpu.get_barrier_semaphore()
    others = [(a, b) for a in range(groups) for b in range(site_devices) if a or b]
    for a, b in others:
        pl.semaphore_signal(
            barrier,
            inc=1,
            device_id={"cls": lax.rem(g + a, groups), "site": lax.rem(me + b, site_devices)},
            device_id_type=MESH,
        )

    copies[0].wait()
    freq = freq_ref[...]
    pi = freq / jnp.sum(freq, axis=1, keepdims=True)
    beta = 1.0 / (1.0 - jnp.sum(pi * pi, axis=1, keepdims=True))
    for i in range(4):
        wide = jnp.broadcast_to(pi[:, i : i + 1], (classes, LANES))
        for c in range(classes):
            stat[c, i] = jnp.broadcast_to(wide[c : c + 1], (8, LANES))
    copies[1].wait()
    lengths = lengths_ref[...]
    r = jnp.exp(beta * lengths) - 1.0
    width = table.shape[1]
    wide_levels = [h for h in range(low) if (local >> h) % LANES == 0]
    tail_start = level_base(taxa, len(wide_levels)) // LANES * LANES
    table[0:classes, 0:branches] = r
    table[0:classes, branches:width] = jnp.zeros((classes, width - branches), f32)
    table[classes : 2 * classes, :] = jnp.zeros((classes, width), f32)
    table[classes : 2 * classes, tail_start : tail_start + 4] = pi
    table[classes : 2 * classes, tail_start + 4 : tail_start + 8] = pi
    tail[...] = table[:, tail_start:width].T
    for c in range(classes):
        pick[c] = jnp.broadcast_to(tail[0:8, classes + c : classes + c + 1], (8, LANES))
    offset = {}
    total_rows = 0
    for h in range(low):
        count = local >> h
        base = level_base(taxa, h)
        offset[h] = total_rows
        if h in wide_levels:
            span = pl.ds(pl.multiple_of(base + g * count, LANES), count)
            columns = table[:, span].T
        else:
            columns = tail[pl.ds(pl.multiple_of(base - tail_start + g * count, 8), count), :]
        for c in range(classes):
            grow[c, total_rows : total_rows + count, :] = jnp.broadcast_to(
                columns[:, c : c + 1], (count, LANES)
            )
        total_rows += count
    copies[2].wait()
    for fetch in fetches:
        fetch.wait()
    flat = codes.reshape(local * folds, LANES)

    def child_row(side, level, node):
        return kids[side, taxa - (taxa >> (level - 1)) + node]

    def factor(c, h, node):
        return grow[c, pl.ds(offset[h] + node, 1), :]

    def tip_codes(tip):
        return flat[pl.ds((tip >> 3) * (8 * folds) + (tip & 7), folds, stride=8), :]

    def spread(c, values, scale):
        mean = (values[0] * stat[c, 0] + values[1] * stat[c, 1]) + (
            values[2] * stat[c, 2] + values[3] * stat[c, 3]
        )
        move = scale * mean
        return [value + move for value in values], mean

    per = [(local >> h) // clades for h in range(low + 1)]
    span = classes // PIECES

    def step(index, carry):
        p = index // clades
        j = lax.rem(index, clades)
        mine = [span * p + n for n in range(span)]
        for n in range(per[1]):
            node = j * per[1] + n
            left = child_row(0, 1, g * (local >> 1) + node) & (local - 1)
            right = child_row(1, 1, g * (local >> 1) + node) & (local - 1)
            a = tip_codes(left)
            b = tip_codes(right)
            same = jnp.where(a == b, 1.0, 0.0)
            in_a = [a == i for i in range(4)]
            in_b = [b == i for i in range(4)]
            for q, c in enumerate(mine):
                pi_a = look_up(pick[c], a)
                pi_b = look_up(pick[c], b)
                off_a = factor(c, 0, left) * pi_a
                off_b = factor(c, 0, right) * pi_b
                on_b = off_b + same
                mean = off_a * (pi_b + off_b) + pi_a * on_b
                move = factor(c, 1, node) * mean
                at_a = (off_a + 1.0) * on_b + move
                at_b = (off_b + 1.0) * (off_a + same) + move
                rest = off_a * off_b + move
                for i in range(4):
                    pairs[n, 4 * q + i] = jnp.where(
                        in_a[i], at_a, jnp.where(in_b[i], at_b, rest)
                    )
        logs = [None] * span
        for n in range(per[3]):
            node = j * per[3] + n
            seconds = [
                child_row(side, 3, g * (local >> 3) + node) & (per[2] - 1) for side in (0, 1)
            ]
            firsts = [
                [
                    child_row(side, 2, g * (local >> 2) + j * per[2] + second) & (per[1] - 1)
                    for side in (0, 1)
                ]
                for second in seconds
            ]
            for q, c in enumerate(mine):
                both = []
                for second, first in zip(seconds, firsts):
                    values = [
                        pairs[first[0], 4 * q + i] * pairs[first[1], 4 * q + i] for i in range(4)
                    ]
                    both.append(spread(c, values, factor(c, 2, j * per[2] + second))[0])
                values = [x * y for x, y in zip(*both)]
                values, mean = spread(c, values, factor(c, 3, node))
                scale = pl.reciprocal(mean, approx=True)
                logs[q] = jnp.log(scale) if n == 0 else logs[q] + jnp.log(scale)
                for i in range(4):
                    mids[n, 4 * q + i] = values[i] * scale
        fourths = [
            [child_row(side, 5, g * (local >> 5) + j * per[5] + n) & (per[4] - 1) for side in (0, 1)]
            for n in range(per[5])
        ]
        thirds = [
            [
                [
                    child_row(side, 4, g * (local >> 4) + j * per[4] + fourth) & (per[3] - 1)
                    for side in (0, 1)
                ]
                for fourth in pair
            ]
            for pair in fourths
        ]
        for q, c in enumerate(mine):
            top = []
            for n in range(per[5]):
                both = []
                for fourth, third in zip(fourths[n], thirds[n]):
                    values = [
                        mids[third[0], 4 * q + i] * mids[third[1], 4 * q + i] for i in range(4)
                    ]
                    both.append(spread(c, values, factor(c, 4, j * per[4] + fourth))[0])
                values = [x * y for x, y in zip(*both)]
                top.append(spread(c, values, factor(c, 5, j * per[5] + n))[0])
            values = [x * y for x, y in zip(*top)]
            inverse = 1.0 / values[3]
            for i in range(3):
                ratio = values[i] * inverse
                for block in range(groups):
                    sent[block, p, j, i, halves * q : halves * (q + 1), :] = ratio[
                        halves * block : halves * (block + 1)
                    ]
            before = jnp.where(j == 0, 0.0, scale_sum[q])
            total = before + (jnp.log(values[3]) - logs[q])
            scale_sum[q] = total
            for block in range(groups):
                sent_scale[block, p, halves * q : halves * (q + 1), :] = total[
                    halves * block : halves * (block + 1)
                ]

        @pl.when(index == 0)
        def _():
            pl.semaphore_wait(barrier, len(others))

        for slot in order:
            target = partner(slot)
            pltpu.make_async_remote_copy(
                src_ref=sent.at[target, p, j],
                dst_ref=got.at[slot, p, j],
                send_sem=send_sem,
                recv_sem=recv_sem,
                device_id={"cls": target},
                device_id_type=MESH,
            ).start()

        @pl.when(j == clades - 1)
        def _():
            for slot in order:
                target = partner(slot)
                pltpu.make_async_remote_copy(
                    src_ref=sent_scale.at[target, p],
                    dst_ref=got_scale.at[slot, p],
                    send_sem=scale_send,
                    recv_sem=scale_recv,
                    device_id={"cls": target},
                    device_id_type=MESH,
                ).start()

        return carry

    xor = groups & (groups - 1) == 0
    order = [2, 3, 1] if groups == 4 else list(range(1, groups))

    def partner(slot):
        return g ^ slot if xor else lax.rem(g + slot, groups)

    def slot_of(source):
        return g ^ source if xor else lax.rem(source + groups - g, groups)

    lax.fori_loop(0, PIECES * clades, step, 0)
    got[0] = sent[g]
    got_scale[0] = sent_scale[g]
    first_up = level_base(taxa, low)
    window = first_up // LANES * LANES
    r8 = jnp.concatenate([r[n // halves : n // halves + 1, window:] for n in range(rows)], axis=0)
    for j in range(branches - first_up):
        at = first_up - window + j
        grow_up[j] = jnp.broadcast_to(r8[:, at : at + 1], (rows, LANES))
    drift = beta * jnp.sum(lengths, axis=1, keepdims=True)
    for copy in copies[3:]:
        copy.wait()
    arrived = got.at[pl.ds(1, groups - 1)]
    pltpu.make_async_copy(arrived, arrived, recv_sem).wait()
    scales_arrived = got_scale.at[pl.ds(1, groups - 1)]
    pltpu.make_async_copy(scales_arrived, scales_arrived, scale_recv).wait()

    def whole(*parts):
        return parts[0] if len(parts) == 1 else jnp.concatenate(parts, axis=0)

    pis8 = [
        jnp.concatenate([stat[n // halves, i, 0:1] for n in range(rows)], axis=0) for i in range(4)
    ]
    scales = functools.reduce(jnp.add, [whole(*[got_scale[k, p] for p in range(PIECES)]) for k in range(groups)])

    def child(tree_level, ident):
        if tree_level == low:
            place = (ident - first_up) & (2**TOP - 1)
            k = slot_of(place // clades)
            j = lax.rem(place, clades)
            values = [whole(*[got[k, p, j, i] for p in range(PIECES)]) for i in range(3)]
            values.append(jnp.ones((rows, LANES), f32))
        else:
            at = jnp.clip(ident - level_base(taxa, low + 1), 0, 2**TOP - 1)
            values = [upper[at, i] for i in range(4)]
        mean = (values[0] * pis8[0] + values[1] * pis8[1]) + (
            values[2] * pis8[2] + values[3] * pis8[3]
        )
        move = grow_up[jnp.clip(ident - first_up, 0, branches - first_up - 1)] * mean
        return [value + move for value in values]

    place = 0
    for tree_level in range(low, LEVELS):
        count = taxa >> (tree_level + 1)
        first = taxa - (taxa >> tree_level)
        for n in range(count):
            left = child(tree_level, kids[0, first + n])
            right = child(tree_level, kids[1, first + n])
            values = [a * b for a, b in zip(left, right)]
            largest = jnp.maximum(
                jnp.maximum(values[0], values[1]), jnp.maximum(values[2], values[3])
            )
            scale = pl.reciprocal(largest, approx=True)
            scales = scales - jnp.log(scale)
            values = [value * scale for value in values]
            if tree_level < LEVELS - 1:
                for i in range(4):
                    upper[place, i] = values[i]
                place += 1
    end = (values[0] * pis8[0] + values[1] * pis8[1]) + (
        values[2] * pis8[2] + values[3] * pis8[3]
    )
    spot = lax.broadcasted_iota(jnp.int32, (classes, classes), 0)
    spot = spot == lax.broadcasted_iota(jnp.int32, (classes, classes), 1)
    weights = jnp.sum(jnp.where(spot, weights_ref[...], 0.0), axis=1, keepdims=True)
    log_weight = jnp.log(weights / jnp.sum(weights, axis=0, keepdims=True))
    bias = log_weight - drift
    bias = jnp.concatenate([bias[n // halves : n // halves + 1] for n in range(rows)], axis=0)
    shifted = scales + jnp.log(end) + bias
    each = [shifted[halves * c : halves * (c + 1)] for c in range(classes)]
    top = functools.reduce(jnp.maximum, each)
    total = top + jnp.log(functools.reduce(jnp.add, [jnp.exp(a - top) for a in each]))
    result[0:halves, :] = total / taxa
    n = counts[pl.ds(g * halves, halves), :].astype(f32)

    def over_halves(x):
        return functools.reduce(jnp.add, [x[h : h + 1] for h in range(halves)])

    loglik = over_halves(n * total)
    seen = over_halves(n)
    sums = [over_halves(n * jnp.exp(a - total)) for a in each] + [loglik, seen]
    size = len(sums)
    sums = jnp.sum(jnp.concatenate(sums, axis=0), axis=1, keepdims=True)
    lane = lax.broadcasted_iota(jnp.int32, (size, LANES), 1)
    spot = lane == lax.broadcasted_iota(jnp.int32, (size, LANES), 0)
    part[...] = jnp.sum(jnp.where(spot, sums, 0.0), axis=0, keepdims=True)
    own = g * site_devices + me
    for a, b in reversed(others):
        pltpu.make_async_remote_copy(
            src_ref=part,
            dst_ref=part_got.at[own],
            send_sem=part_send,
            recv_sem=part_recv,
            device_id={"cls": lax.rem(g + a, groups), "site": lax.rem(me + b, site_devices)},
            device_id_type=MESH,
        ).start()
    part_got[own] = part[...]
    arrivals = part_got.at[pl.ds(0, len(others))]
    pltpu.make_async_copy(arrivals, arrivals, part_recv).wait()
    line = [part_got[d] for d in range(groups * site_devices)]
    while len(line) > 1:
        line = [jnp.add(*line[d : d + 2]) if d + 1 < len(line) else line[d] for d in range(0, len(line), 2)]
    lane = lax.broadcasted_iota(jnp.int32, (3, LANES), 1)
    row = lax.broadcasted_iota(jnp.int32, (3, LANES), 0)
    spot = lane == jnp.where(row == 0, g, classes - 1 + row)
    line = jnp.sum(jnp.where(spot, line[0], 0.0), axis=1, keepdims=True)
    all_count = line[2:3]
    mean = line[1:2] / (all_count * taxa)
    share = line[0:1] / all_count
    pltpu.make_async_copy(arrivals, arrivals, part_send).wait()
    pltpu.make_async_copy(arrived, arrived, send_sem).wait()
    pltpu.make_async_copy(scales_arrived, scales_arrived, scale_send).wait()
    result[halves : halves + 1, :] = jnp.broadcast_to(share, (1, LANES))
    result[halves + 1 : halves + 2, :] = jnp.broadcast_to(mean, (1, LANES))


def finish(result, site_out, weight_out, mean_out):
    halves = result.shape[0] - 2
    for half in range(halves):
        site_out[0:1, half * LANES : (half + 1) * LANES] = result[half : half + 1, :]
    weight_out[...] = result[halves : halves + 1, 0:1]
    mean_out[...] = result[halves + 1 : halves + 2, 0:1]


def solution(mesh):
    groups = mesh.shape["cls"]
    site_devices = mesh.shape["site"]

    def per_device(tip_codes, counts, children, lengths, frequencies, weights):
        local, sites = tip_codes.shape
        taxa = local * groups
        classes, branches = lengths.shape
        quarter = sites // groups
        halves = quarter // LANES
        rows = halves * classes
        low = LEVELS - TOP
        clades = local >> low
        low_rows = sum(local >> h for h in range(low))
        table_width = -(-branches // LANES) * LANES
        wide_levels = [h for h in range(low) if (local >> h) % LANES == 0]
        tail_start = level_base(taxa, len(wide_levels)) // LANES * LANES
        folds = sites // LANES
        up_count = branches - level_base(taxa, low)
        kids = children.T
        vmem = pl.BlockSpec(memory_space=pltpu.VMEM)
        hbm = pl.BlockSpec(memory_space=pltpu.HBM)
        f32 = jnp.float32
        result = pl.pallas_call(
            functools.partial(kernel, groups, site_devices),
            out_shape=jax.ShapeDtypeStruct((halves + 2, LANES), f32),
            in_specs=[hbm] * 6,
            out_specs=vmem,
            scratch_shapes=[
                pltpu.VMEM((local // 8, folds, 8, LANES), jnp.int32),
                pltpu.VMEM((folds, LANES), jnp.int32),
                pltpu.SMEM(kids.shape, jnp.int32),
                pltpu.VMEM(lengths.shape, f32),
                pltpu.VMEM(frequencies.shape, f32),
                pltpu.VMEM((1, classes), f32),
                pltpu.VMEM((8, table_width), f32),
                pltpu.VMEM((table_width - tail_start, 8), f32),
                pltpu.VMEM((classes, low_rows, LANES), f32),
                pltpu.VMEM((up_count, rows, LANES), f32),
                pltpu.VMEM((classes, 4, 8, LANES), f32),
                pltpu.VMEM((classes, 8, LANES), f32),
                pltpu.VMEM(((local >> 1) // clades, 4 * classes // PIECES, folds, LANES), f32),
                pltpu.VMEM(((local >> 3) // clades, 4 * classes // PIECES, folds, LANES), f32),
                pltpu.VMEM((classes // PIECES, folds, LANES), f32),
                pltpu.VMEM((groups, PIECES, clades, 3, rows // PIECES, LANES), f32),
                pltpu.VMEM((groups, PIECES, clades, 3, rows // PIECES, LANES), f32),
                pltpu.VMEM((groups, PIECES, rows // PIECES, LANES), f32),
                pltpu.VMEM((groups, PIECES, rows // PIECES, LANES), f32),
                pltpu.VMEM((2 ** TOP, 4, rows, LANES), f32),
                pltpu.VMEM((1, LANES), f32),
                pltpu.VMEM((groups * site_devices, 1, LANES), f32),
                pltpu.SemaphoreType.DMA((5,)),
                pltpu.SemaphoreType.DMA((folds,)),
                pltpu.SemaphoreType.DMA,
                pltpu.SemaphoreType.DMA,
                pltpu.SemaphoreType.DMA,
                pltpu.SemaphoreType.DMA,
                pltpu.SemaphoreType.DMA,
                pltpu.SemaphoreType.DMA,
            ],
            compiler_params=pltpu.CompilerParams(collective_id=0, has_side_effects=True, vmem_limit_bytes=56549376),
        )(
            tip_codes.reshape(local // 8, 8, sites),
            counts.reshape(folds, LANES),
            kids,
            lengths,
            frequencies,
            weights.reshape(1, classes),
        )
        site_loglik, new_weights, mean_loglik = pl.pallas_call(
            finish,
            out_shape=(
                jax.ShapeDtypeStruct((1, quarter), f32),
                jax.ShapeDtypeStruct((1, 1), f32),
                jax.ShapeDtypeStruct((1, 1), f32),
            ),
            in_specs=[vmem],
            out_specs=(vmem, vmem, vmem),
            compiler_params=pltpu.CompilerParams(vmem_limit_bytes=1 << 20),
        )(result)
        return site_loglik, new_weights.reshape(1), mean_loglik.reshape(())

    return jax.shard_map(
        per_device,
        mesh=mesh,
        in_specs=(P("cls", "site"), P("site"), P(), P(), P(), P()),
        out_specs=(P("cls", "site"), P("cls"), P()),
        check_vma=False,
    )
```

time: 22.4 us -> 20.4 us (0.911)
  Pallas kernels: 21.6 us -> 18.9 us
  local copies, waits for them, and re-layouts: 0 us -> 0.65 us
    pallas_call x1, Pallas kernels: 20.3 us -> 18.3 us  [per_device(): pl.pallas_call(functools.partial(kernel, groups, site_devices), out_shape...]
    pallas_call x1, Pallas kernels: 1.24 us -> 0.57 us  [per_device(): pl.pallas_call(finish, out_shape=(jax.ShapeDtypeStruct((1, quarter), f32)...]
    unnamed x0 -> x2, local copies, waits for them, and re-layouts: none -> 0.65 us
where the time goes in v2:
time: 20.4 us; the launch traced here: 20.2 us
  Pallas kernels  18.9 us (93%)
  local copies, waits for them, and re-layouts  0.65 us (3%)
  between operations  0.65 us (3%)
    pallas_call x1, Pallas kernels, per_device(): pl.pallas_call(functools.partial(kernel, groups, site_devices), out_shape...  18.3 us
    unnamed x2, local copies, waits for them, and re-layouts  0.65 us
    pallas_call x1, Pallas kernels, per_device(): pl.pallas_call(finish, out_shape=(jax.ShapeDtypeStruct((1, quarter), f32)...  0.57 us

profile of v2, /device:TPU:0, one launch (start us, length us, event | category | flops | bytes accessed | tf_op | source)
XLA Modules:
  0.0 20.2 jit_solution(15207159016242252955)
XLA Ops:
  0.6 0.0 copy-start
  0.6 0.6 %copy-done = f32[4]{0:T(128)S(1)} copy-done((f32[4]{0:T(128)S(1)}, f32[4]{0:T(128)}, u32[]{:S(2)}) %copy-start) | copy-done | bytes 40
  1.3 18.3 %shard_map.85.result = f32[4,128]{1,0:T(4,128)S(1)} custom-call(s32[32,8,1024]{2,1,0:T(8,128)} %bitcast.7, s32[8,128]{1,0:T(8,128)} %bitcast.9, s32[2,1023]{1,0:T(2,128)} %bitcast.8, f32[4,2046]{1,0:T(4,128)} %lengths_hbm.1, f32[4,4]{1,0:T(4,128)} %freq_hbm.1, f32[1,4]{1,0:T(1,128)S(1)} %bitcast.6), custom_call_target="tpu_custom_call" | custom-call | tf_op jit(solution)/shard_map/pallas_call | solution.py:463
  19.6 0.6 %shard_map.86 = (f32[1,256]{1,0:T(1,128)}, f32[1,1]{1,0:T(1,128)}, f32[1,1]{1,0:T(1,128)}) custom-call(f32[4,128]{1,0:T(4,128)S(1)} %shard_map.85.result), custom_call_target="tpu_custom_call" | custom-call | tf_op jit(solution)/shard_map/pallas_call | solution.py:509
Async XLA Ops:
  0.6 0.7 %copy-start = (f32[4]{0:T(128)S(1)}, f32[4]{0:T(128)}, u32[]{:S(2)}) copy-start(f32[4]{0:T(128)} %param.11) | copy-start | bytes 52

commit v3 on v2

--- a/solution.py
+++ b/solution.py
@@ -52,6 +52,7 @@
     freq_ref,
     weights_ref,
     table,
+    columns,
     tail,
     grow,
     grow_up,
@@ -118,43 +119,47 @@
         )
 
     copies[0].wait()
-    freq = freq_ref[...]
-    pi = freq / jnp.sum(freq, axis=1, keepdims=True)
-    beta = 1.0 / (1.0 - jnp.sum(pi * pi, axis=1, keepdims=True))
-    for i in range(4):
-        wide = jnp.broadcast_to(pi[:, i : i + 1], (classes, LANES))
-        for c in range(classes):
-            stat[c, i] = jnp.broadcast_to(wide[c : c + 1], (8, LANES))
+    freq = [jnp.broadcast_to(freq_ref[:, i : i + 1], (classes, LANES)) for i in range(4)]
+    whole_freq = (freq[0] + freq[1]) + (freq[2] + freq[3])
+    pi = [own / whole_freq for own in freq]
+    beta = 1.0 / (1.0 - ((pi[0] * pi[0] + pi[1] * pi[1]) + (pi[2] * pi[2] + pi[3] * pi[3])))
+    width = table.shape[1]
+    table[classes:8, :] = jnp.zeros((8 - classes, width), f32)
+    for c in range(classes):
+        for i in range(4):
+            stat[c, i] = jnp.broadcast_to(pi[i][c : c + 1], (8, LANES))
+            pick[c, i : i + 1] = pi[i][c : c + 1]
+            pick[c, i + 4 : i + 5] = pi[i][c : c + 1]
     copies[1].wait()
-    lengths = lengths_ref[...]
-    r = jnp.exp(beta * lengths) - 1.0
-    width = table.shape[1]
+    for at in range(0, width, LANES):
+        end = min(at + LANES, branches)
+        table[0:classes, at:end] = jnp.exp(beta[:, : end - at] * lengths_ref[:, at:end]) - 1.0
     wide_levels = [h for h in range(low) if (local >> h) % LANES == 0]
     tail_start = level_base(taxa, len(wide_levels)) // LANES * LANES
-    table[0:classes, 0:branches] = r
-    table[0:classes, branches:width] = jnp.zeros((classes, width - branches), f32)
-    table[classes : 2 * classes, :] = jnp.zeros((classes, width), f32)
-    table[classes : 2 * classes, tail_start : tail_start + 4] = pi
-    table[classes : 2 * classes, tail_start + 4 : tail_start + 8] = pi
-    tail[...] = table[:, tail_start:width].T
-    for c in range(classes):
-        pick[c] = jnp.broadcast_to(tail[0:8, classes + c : classes + c + 1], (8, LANES))
     offset = {}
     total_rows = 0
     for h in range(low):
         count = local >> h
-        base = level_base(taxa, h)
         offset[h] = total_rows
         if h in wide_levels:
-            span = pl.ds(pl.multiple_of(base + g * count, LANES), count)
-            columns = table[:, span].T
+            here = pl.ds(pl.multiple_of(level_base(taxa, h) + g * count, LANES), count)
+            columns[total_rows : total_rows + count, :] = table[:, here].T
+        total_rows += count
+    tail[...] = table[:, tail_start:width].T
+    per = [(local >> h) // clades for h in range(low + 1)]
+
+    def fill(h, start, count):
+        if h in wide_levels:
+            column = columns[pl.ds(pl.multiple_of(offset[h] + start, 8), count), :]
         else:
-            columns = tail[pl.ds(pl.multiple_of(base - tail_start + g * count, 8), count), :]
+            base = level_base(taxa, h) - tail_start + g * (local >> h)
+            column = tail[pl.ds(pl.multiple_of(base + start, 8), count), :]
+        target = pl.ds(pl.multiple_of(offset[h] + start, 8), count)
         for c in range(classes):
-            grow[c, total_rows : total_rows + count, :] = jnp.broadcast_to(
-                columns[:, c : c + 1], (count, LANES)
-            )
-        total_rows += count
+            grow[c, target, :] = jnp.broadcast_to(column[:, c : c + 1], (count, LANES))
+
+    for h in range(low):
+        fill(h, 0, local >> h)
     copies[2].wait()
     for fetch in fetches:
         fetch.wait()
@@ -176,7 +181,6 @@
         move = scale * mean
         return [value + move for value in values], mean
 
-    per = [(local >> h) // clades for h in range(low + 1)]
     span = classes // PIECES
 
     def step(index, carry):
@@ -318,13 +322,27 @@
     got_scale[0] = sent_scale[g]
     first_up = level_base(taxa, low)
     window = first_up // LANES * LANES
-    r8 = jnp.concatenate([r[n // halves : n // halves + 1, window:] for n in range(rows)], axis=0)
+    r8 = jnp.concatenate([table[n // halves : n // halves + 1, window:branches] for n in range(rows)], axis=0)
     for j in range(branches - first_up):
         at = first_up - window + j
         grow_up[j] = jnp.broadcast_to(r8[:, at : at + 1], (rows, LANES))
-    drift = beta * jnp.sum(lengths, axis=1, keepdims=True)
+    drift = beta[:, 0:1] * jnp.sum(lengths_ref[...], axis=1, keepdims=True)
     for copy in copies[3:]:
         copy.wait()
+    pis8 = [
+        jnp.concatenate([stat[n // halves, i, 0:1] for n in range(rows)], axis=0) for i in range(4)
+    ]
+    spot = lax.broadcasted_iota(jnp.int32, (classes, classes), 0)
+    spot = spot == lax.broadcasted_iota(jnp.int32, (classes, classes), 1)
+    weights = jnp.sum(jnp.where(spot, weights_ref[...], 0.0), axis=1, keepdims=True)
+    log_weight = jnp.log(weights / jnp.sum(weights, axis=0, keepdims=True))
+    bias = log_weight - drift
+    bias = jnp.concatenate([bias[n // halves : n // halves + 1] for n in range(rows)], axis=0)
+    seen_at = counts[pl.ds(g * halves, halves), :].astype(f32)
+    def over_halves(x):
+        return functools.reduce(jnp.add, [x[h : h + 1] for h in range(halves)])
+
+    seen = over_halves(seen_at)
     arrived = got.at[pl.ds(1, groups - 1)]
     pltpu.make_async_copy(arrived, arrived, recv_sem).wait()
     scales_arrived = got_scale.at[pl.ds(1, groups - 1)]
@@ -333,9 +351,6 @@
     def whole(*parts):
         return parts[0] if len(parts) == 1 else jnp.concatenate(parts, axis=0)
 
-    pis8 = [
-        jnp.concatenate([stat[n // halves, i, 0:1] for n in range(rows)], axis=0) for i in range(4)
-    ]
     scales = functools.reduce(jnp.add, [whole(*[got_scale[k, p] for p in range(PIECES)]) for k in range(groups)])
 
     def child(tree_level, ident):
@@ -375,25 +390,14 @@
     end = (values[0] * pis8[0] + values[1] * pis8[1]) + (
         values[2] * pis8[2] + values[3] * pis8[3]
     )
-    spot = lax.broadcasted_iota(jnp.int32, (classes, classes), 0)
-    spot = spot == lax.broadcasted_iota(jnp.int32, (classes, classes), 1)
-    weights = jnp.sum(jnp.where(spot, weights_ref[...], 0.0), axis=1, keepdims=True)
-    log_weight = jnp.log(weights / jnp.sum(weights, axis=0, keepdims=True))
-    bias = log_weight - drift
-    bias = jnp.concatenate([bias[n // halves : n // halves + 1] for n in range(rows)], axis=0)
     shifted = scales + jnp.log(end) + bias
     each = [shifted[halves * c : halves * (c + 1)] for c in range(classes)]
     top = functools.reduce(jnp.maximum, each)
     total = top + jnp.log(functools.reduce(jnp.add, [jnp.exp(a - top) for a in each]))
     result[0:halves, :] = total / taxa
-    n = counts[pl.ds(g * halves, halves), :].astype(f32)
-
-    def over_halves(x):
-        return functools.reduce(jnp.add, [x[h : h + 1] for h in range(halves)])
-
-    loglik = over_halves(n * total)
-    seen = over_halves(n)
-    sums = [over_halves(n * jnp.exp(a - total)) for a in each] + [loglik, seen]
+
+    loglik = over_halves(seen_at * total)
+    sums = [over_halves(seen_at * jnp.exp(a - total)) for a in each] + [loglik, seen]
     size = len(sums)
     sums = jnp.sum(jnp.concatenate(sums, axis=0), axis=1, keepdims=True)
     lane = lax.broadcasted_iota(jnp.int32, (size, LANES), 1)
@@ -473,6 +477,7 @@
                 pltpu.VMEM(frequencies.shape, f32),
                 pltpu.VMEM((1, classes), f32),
                 pltpu.VMEM((8, table_width), f32),
+                pltpu.VMEM((sum(local >> h for h in wide_levels), 8), f32),
                 pltpu.VMEM((table_width - tail_start, 8), f32),
                 pltpu.VMEM((classes, low_rows, LANES), f32),
                 pltpu.VMEM((up_count, rows, LANES), f32),
@@ -497,14 +502,19 @@
                 pltpu.SemaphoreType.DMA,
                 pltpu.SemaphoreType.DMA,
             ],
-            compiler_params=pltpu.CompilerParams(collective_id=0, has_side_effects=True, vmem_limit_bytes=56549376),
+            compiler_params=pltpu.CompilerParams(collective_id=0, has_side_effects=True, vmem_limit_bytes=32 << 20),
         )(
-            tip_codes.reshape(local // 8, 8, sites),
-            counts.reshape(folds, LANES),
-            kids,
-            lengths,
-            frequencies,
-            weights.reshape(1, classes),
+            *(
+                pltpu.with_memory_space_constraint(operand, pltpu.HBM)
+                for operand in (
+                    tip_codes.reshape(local // 8, 8, sites),
+                    counts.reshape(folds, LANES),
+                    kids,
+                    lengths,
+                    frequencies,
+                    weights.reshape(1, classes),
+                )
+            )
         )
         site_loglik, new_weights, mean_loglik = pl.pallas_call(
             finish,

time: 20.4 us -> 19.6 us (0.961)
  local copies, waits for them, and re-layouts: 0.65 us -> 0 us
    unnamed x2 -> x0, local copies, waits for them, and re-layouts: 0.65 us -> none
where the time goes in v3:
time: 19.6 us; the launch traced here: 19.5 us
  Pallas kernels  18.9 us (96%)
  between operations  0.64 us (3%)
    pallas_call x1, Pallas kernels, per_device(): pl.pallas_call(functools.partial(kernel, groups, site_devices), out_shape...  18.3 us
    pallas_call x1, Pallas kernels, per_device(): pl.pallas_call(finish, out_shape=(jax.ShapeDtypeStruct((1, quarter), f32)...  0.57 us

profile of v3, /device:TPU:0, one launch (start us, length us, event | category | flops | bytes accessed | tf_op | source)
XLA Modules:
  0.0 19.5 jit_solution(13754160328945686307)
XLA Ops:
  0.6 18.3 %shard_map.85.result = f32[4,128]{1,0:T(4,128)S(1)} custom-call(s32[32,8,1024]{2,1,0:T(8,128)} %bitcast.6, s32[8,128]{1,0:T(8,128)} %bitcast.8, s32[2,1023]{1,0:T(2,128)} %bitcast.7, f32[4,2046]{1,0:T(4,128)} %lengths_hbm.1, f32[4,4]{1,0:T(4,128)} %freq_hbm.1, f32[1,4]{1,0:T(1,128)} %bitcast.9), custom_call_target="tpu_custom_call" | custom-call | tf_op jit(solution)/shard_map/pallas_call | solution.py:467
  18.9 0.6 %shard_map.86 = (f32[1,256]{1,0:T(1,128)}, f32[1,1]{1,0:T(1,128)}, f32[1,1]{1,0:T(1,128)}) custom-call(f32[4,128]{1,0:T(4,128)S(1)} %shard_map.85.result), custom_call_target="tpu_custom_call" | custom-call | tf_op jit(solution)/shard_map/pallas_call | solution.py:519

commit v4 on v3

--- a/solution.py
+++ b/solution.py
@@ -11,6 +11,7 @@
 TOP = 4
 LANES = 128
 PIECES = 1
+SIDES = 2
 MESH = pl.DeviceIdType.MESH
 
 
@@ -66,8 +67,12 @@
     sent_scale,
     got_scale,
     upper,
+    counts_got,
+    site_sent,
+    site_got,
     part,
     part_got,
+    part_sink,
     in_sem,
     code_sem,
     send_sem,
@@ -76,9 +81,16 @@
     scale_recv,
     part_send,
     part_recv,
+    counts_send,
+    counts_recv,
+    site_send,
+    site_recv,
 ):
     g = lax.axis_index("cls")
     me = lax.axis_index("site")
+    side = lax.rem(me, SIDES)
+    hub = side == SIDES - 1
+    hub_site = me + SIDES - 1 - side
     tiles, folds, _, _ = codes.shape
     local = tiles * 8
     taxa = local * groups
@@ -282,34 +294,40 @@
         def _():
             pl.semaphore_wait(barrier, len(others))
 
+        def to_hub(source, target, slot, send, recv):
+            copy = pltpu.make_async_remote_copy(
+                src_ref=source,
+                dst_ref=target,
+                send_sem=send,
+                recv_sem=recv.at[side],
+                device_id={"cls": partner(slot), "site": hub_site},
+                device_id_type=MESH,
+            )
+            if slot:
+                copy.start()
+            else:
+                pl.when(jnp.logical_not(hub))(copy.start)
+
         for slot in order:
-            target = partner(slot)
-            pltpu.make_async_remote_copy(
-                src_ref=sent.at[target, p, j],
-                dst_ref=got.at[slot, p, j],
-                send_sem=send_sem,
-                recv_sem=recv_sem,
-                device_id={"cls": target},
-                device_id_type=MESH,
-            ).start()
+            to_hub(
+                sent.at[partner(slot), p, j], got.at[slot, p, j, :, side], slot, send_sem, recv_sem
+            )
 
         @pl.when(j == clades - 1)
         def _():
             for slot in order:
-                target = partner(slot)
-                pltpu.make_async_remote_copy(
-                    src_ref=sent_scale.at[target, p],
-                    dst_ref=got_scale.at[slot, p],
-                    send_sem=scale_send,
-                    recv_sem=scale_recv,
-                    device_id={"cls": target},
-                    device_id_type=MESH,
-                ).start()
+                to_hub(
+                    sent_scale.at[partner(slot), p],
+                    got_scale.at[slot, p, side],
+                    slot,
+                    scale_send,
+                    scale_recv,
+                )
 
         return carry
 
     xor = groups & (groups - 1) == 0
-    order = [2, 3, 1] if groups == 4 else list(range(1, groups))
+    order = ([2, 3, 1] if groups == 4 else list(range(1, groups))) + [0]
 
     def partner(slot):
         return g ^ slot if xor else lax.rem(g + slot, groups)
@@ -318,8 +336,22 @@
         return g ^ source if xor else lax.rem(source + groups - g, groups)
 
     lax.fori_loop(0, PIECES * clades, step, 0)
-    got[0] = sent[g]
-    got_scale[0] = sent_scale[g]
+    for p in range(PIECES):
+        for j in range(clades):
+            for i in range(3):
+                got[0, p, j, i, SIDES - 1] = sent[g, p, j, i]
+        got_scale[0, p, SIDES - 1] = sent_scale[g, p]
+    for copy in copies[3:]:
+        copy.wait()
+    counts_copy = pltpu.make_async_remote_copy(
+        src_ref=counts,
+        dst_ref=counts_got,
+        send_sem=counts_send,
+        recv_sem=counts_recv,
+        device_id={"site": hub_site},
+        device_id_type=MESH,
+    )
+    pl.when(jnp.logical_not(hub))(counts_copy.start)
     first_up = level_base(taxa, low)
     window = first_up // LANES * LANES
     r8 = jnp.concatenate([table[n // halves : n // halves + 1, window:branches] for n in range(rows)], axis=0)
@@ -327,8 +359,6 @@
         at = first_up - window + j
         grow_up[j] = jnp.broadcast_to(r8[:, at : at + 1], (rows, LANES))
     drift = beta[:, 0:1] * jnp.sum(lengths_ref[...], axis=1, keepdims=True)
-    for copy in copies[3:]:
-        copy.wait()
     pis8 = [
         jnp.concatenate([stat[n // halves, i, 0:1] for n in range(rows)], axis=0) for i in range(4)
     ]
@@ -338,85 +368,124 @@
     log_weight = jnp.log(weights / jnp.sum(weights, axis=0, keepdims=True))
     bias = log_weight - drift
     bias = jnp.concatenate([bias[n // halves : n // halves + 1] for n in range(rows)], axis=0)
-    seen_at = counts[pl.ds(g * halves, halves), :].astype(f32)
     def over_halves(x):
-        return functools.reduce(jnp.add, [x[h : h + 1] for h in range(halves)])
-
-    seen = over_halves(seen_at)
-    arrived = got.at[pl.ds(1, groups - 1)]
-    pltpu.make_async_copy(arrived, arrived, recv_sem).wait()
-    scales_arrived = got_scale.at[pl.ds(1, groups - 1)]
-    pltpu.make_async_copy(scales_arrived, scales_arrived, scale_recv).wait()
-
-    def whole(*parts):
-        return parts[0] if len(parts) == 1 else jnp.concatenate(parts, axis=0)
-
-    scales = functools.reduce(jnp.add, [whole(*[got_scale[k, p] for p in range(PIECES)]) for k in range(groups)])
-
-    def child(tree_level, ident):
-        if tree_level == low:
-            place = (ident - first_up) & (2**TOP - 1)
-            k = slot_of(place // clades)
-            j = lax.rem(place, clades)
-            values = [whole(*[got[k, p, j, i] for p in range(PIECES)]) for i in range(3)]
-            values.append(jnp.ones((rows, LANES), f32))
-        else:
-            at = jnp.clip(ident - level_base(taxa, low + 1), 0, 2**TOP - 1)
-            values = [upper[at, i] for i in range(4)]
-        mean = (values[0] * pis8[0] + values[1] * pis8[1]) + (
+        return functools.reduce(
+            jnp.add, [x[d, h : h + 1] for d in range(SIDES) for h in range(halves)]
+        )
+
+    sources = groups * (site_devices // SIDES)
+
+    @pl.when(hub)
+    def _():
+        near = got.at[:, :, :, :, 0]
+        far = got.at[pl.ds(1, groups - 1), :, :, :, 1]
+        pltpu.make_async_copy(near, near, recv_sem.at[0]).wait()
+        pltpu.make_async_copy(far, far, recv_sem.at[1]).wait()
+        near = got_scale.at[:, :, 0]
+        far = got_scale.at[pl.ds(1, groups - 1), :, 1]
+        pltpu.make_async_copy(near, near, scale_recv.at[0]).wait()
+        pltpu.make_async_copy(far, far, scale_recv.at[1]).wait()
+        pltpu.make_async_copy(counts_got, counts_got, counts_recv).wait()
+        quarter = pl.ds(g * halves, halves)
+        seen_at = jnp.stack([counts_got[quarter, :], counts[quarter, :]]).astype(f32)
+
+        def whole(*parts):
+            return parts[0] if len(parts) == 1 else jnp.concatenate(parts, axis=0)
+
+        scales = functools.reduce(jnp.add, [whole(*[got_scale[k, p] for p in range(PIECES)]) for k in range(groups)])
+
+        def child(tree_level, ident):
+            if tree_level == low:
+                place = (ident - first_up) & (2**TOP - 1)
+                k = slot_of(place // clades)
+                j = lax.rem(place, clades)
+                values = [whole(*[got[k, p, j, i] for p in range(PIECES)]) for i in range(3)]
+                values.append(jnp.ones((SIDES, rows, LANES), f32))
+            else:
+                at = jnp.clip(ident - level_base(taxa, low + 1), 0, 2**TOP - 1)
+                values = [upper[at, i] for i in range(4)]
+            mean = (values[0] * pis8[0] + values[1] * pis8[1]) + (
+                values[2] * pis8[2] + values[3] * pis8[3]
+            )
+            move = grow_up[jnp.clip(ident - first_up, 0, branches - first_up - 1)] * mean
+            return [value + move for value in values]
+
+        place = 0
+        for tree_level in range(low, LEVELS):
+            count = taxa >> (tree_level + 1)
+            first = taxa - (taxa >> tree_level)
+            for n in range(count):
+                left = child(tree_level, kids[0, first + n])
+                right = child(tree_level, kids[1, first + n])
+                values = [a * b for a, b in zip(left, right)]
+                largest = jnp.maximum(
+                    jnp.maximum(values[0], values[1]), jnp.maximum(values[2], values[3])
+                )
+                scale = pl.reciprocal(largest, approx=True)
+                scales = scales - jnp.log(scale)
+                values = [value * scale for value in values]
+                if tree_level < LEVELS - 1:
+                    for i in range(4):
+                        upper[place, i] = values[i]
+                    place += 1
+        end = (values[0] * pis8[0] + values[1] * pis8[1]) + (
             values[2] * pis8[2] + values[3] * pis8[3]
         )
-        move = grow_up[jnp.clip(ident - first_up, 0, branches - first_up - 1)] * mean
-        return [value + move for value in values]
-
-    place = 0
-    for tree_level in range(low, LEVELS):
-        count = taxa >> (tree_level + 1)
-        first = taxa - (taxa >> tree_level)
-        for n in range(count):
-            left = child(tree_level, kids[0, first + n])
-            right = child(tree_level, kids[1, first + n])
-            values = [a * b for a, b in zip(left, right)]
-            largest = jnp.maximum(
-                jnp.maximum(values[0], values[1]), jnp.maximum(values[2], values[3])
-            )
-            scale = pl.reciprocal(largest, approx=True)
-            scales = scales - jnp.log(scale)
-            values = [value * scale for value in values]
-            if tree_level < LEVELS - 1:
-                for i in range(4):
-                    upper[place, i] = values[i]
-                place += 1
-    end = (values[0] * pis8[0] + values[1] * pis8[1]) + (
-        values[2] * pis8[2] + values[3] * pis8[3]
-    )
-    shifted = scales + jnp.log(end) + bias
-    each = [shifted[halves * c : halves * (c + 1)] for c in range(classes)]
-    top = functools.reduce(jnp.maximum, each)
-    total = top + jnp.log(functools.reduce(jnp.add, [jnp.exp(a - top) for a in each]))
-    result[0:halves, :] = total / taxa
-
-    loglik = over_halves(seen_at * total)
-    sums = [over_halves(seen_at * jnp.exp(a - total)) for a in each] + [loglik, seen]
-    size = len(sums)
-    sums = jnp.sum(jnp.concatenate(sums, axis=0), axis=1, keepdims=True)
-    lane = lax.broadcasted_iota(jnp.int32, (size, LANES), 1)
-    spot = lane == lax.broadcasted_iota(jnp.int32, (size, LANES), 0)
-    part[...] = jnp.sum(jnp.where(spot, sums, 0.0), axis=0, keepdims=True)
-    own = g * site_devices + me
-    for a, b in reversed(others):
-        pltpu.make_async_remote_copy(
-            src_ref=part,
-            dst_ref=part_got.at[own],
-            send_sem=part_send,
-            recv_sem=part_recv,
-            device_id={"cls": lax.rem(g + a, groups), "site": lax.rem(me + b, site_devices)},
+        shifted = scales + jnp.log(end) + bias
+        each = [shifted[:, halves * c : halves * (c + 1)] for c in range(classes)]
+        top = functools.reduce(jnp.maximum, each)
+        total = top + jnp.log(functools.reduce(jnp.add, [jnp.exp(a - top) for a in each]))
+        site_sent[...] = total[0] / taxa
+
+        loglik = over_halves(seen_at * total)
+        seen = over_halves(seen_at)
+        sums = [over_halves(seen_at * jnp.exp(a - total)) for a in each] + [loglik, seen]
+        size = len(sums)
+        sums = jnp.sum(jnp.concatenate(sums, axis=0), axis=1, keepdims=True)
+        lane = lax.broadcasted_iota(jnp.int32, (size, LANES), 1)
+        spot = lane == lax.broadcasted_iota(jnp.int32, (size, LANES), 0)
+        part[...] = jnp.sum(jnp.where(spot, sums, 0.0), axis=0, keepdims=True)
+        own = g * (site_devices // SIDES) + me // SIDES
+        site_copy = pltpu.make_async_remote_copy(
+            src_ref=site_sent,
+            dst_ref=site_got,
+            send_sem=site_send,
+            recv_sem=site_recv,
+            device_id={"site": me + 1 - SIDES},
             device_id_type=MESH,
-        ).start()
-    part_got[own] = part[...]
-    arrivals = part_got.at[pl.ds(0, len(others))]
-    pltpu.make_async_copy(arrivals, arrivals, part_recv).wait()
-    line = [part_got[d] for d in range(groups * site_devices)]
+        )
+        site_copy.start()
+        for a, b in reversed(others):
+            pltpu.make_async_remote_copy(
+                src_ref=part,
+                dst_ref=part_got.at[own],
+                send_sem=part_send,
+                recv_sem=part_recv,
+                device_id={"cls": lax.rem(g + a, groups), "site": lax.rem(me + b, site_devices)},
+                device_id_type=MESH,
+            ).start()
+        part_got[own] = part[...]
+        result[0:halves, :] = total[SIDES - 1] / taxa
+        rest = part_got.at[pl.ds(0, sources - 1)]
+        pltpu.make_async_copy(rest, rest, part_recv).wait()
+        sends = part_sink.at[pl.ds(0, len(others))]
+        pltpu.make_async_copy(sends, sends, part_send).wait()
+        site_copy.wait_send()
+        done = sent.at[pl.ds(0, groups - 1)]
+        pltpu.make_async_copy(done, done, send_sem).wait()
+        done = sent_scale.at[pl.ds(0, groups - 1)]
+        pltpu.make_async_copy(done, done, scale_send).wait()
+
+    @pl.when(jnp.logical_not(hub))
+    def _():
+        counts_copy.wait_send()
+        pltpu.make_async_copy(sent, sent, send_sem).wait()
+        pltpu.make_async_copy(sent_scale, sent_scale, scale_send).wait()
+        pltpu.make_async_copy(site_got, site_got, site_recv).wait()
+        result[0:halves, :] = site_got[...]
+        pltpu.make_async_copy(part_got, part_got, part_recv).wait()
+
+    line = [part_got[d] for d in range(sources)]
     while len(line) > 1:
         line = [jnp.add(*line[d : d + 2]) if d + 1 < len(line) else line[d] for d in range(0, len(line), 2)]
     lane = lax.broadcasted_iota(jnp.int32, (3, LANES), 1)
@@ -426,9 +495,6 @@
     all_count = line[2:3]
     mean = line[1:2] / (all_count * taxa)
     share = line[0:1] / all_count
-    pltpu.make_async_copy(arrivals, arrivals, part_send).wait()
-    pltpu.make_async_copy(arrived, arrived, send_sem).wait()
-    pltpu.make_async_copy(scales_arrived, scales_arrived, scale_send).wait()
     result[halves : halves + 1, :] = jnp.broadcast_to(share, (1, LANES))
     result[halves + 1 : halves + 2, :] = jnp.broadcast_to(mean, (1, LANES))
 
@@ -487,14 +553,22 @@
                 pltpu.VMEM(((local >> 3) // clades, 4 * classes // PIECES, folds, LANES), f32),
                 pltpu.VMEM((classes // PIECES, folds, LANES), f32),
                 pltpu.VMEM((groups, PIECES, clades, 3, rows // PIECES, LANES), f32),
-                pltpu.VMEM((groups, PIECES, clades, 3, rows // PIECES, LANES), f32),
+                pltpu.VMEM((groups, PIECES, clades, 3, SIDES, rows // PIECES, LANES), f32),
                 pltpu.VMEM((groups, PIECES, rows // PIECES, LANES), f32),
-                pltpu.VMEM((groups, PIECES, rows // PIECES, LANES), f32),
-                pltpu.VMEM((2 ** TOP, 4, rows, LANES), f32),
+                pltpu.VMEM((groups, PIECES, SIDES, rows // PIECES, LANES), f32),
+                pltpu.VMEM((2 ** TOP, 4, SIDES, rows, LANES), f32),
+                pltpu.VMEM((folds, LANES), jnp.int32),
+                pltpu.VMEM((halves, LANES), f32),
+                pltpu.VMEM((halves, LANES), f32),
                 pltpu.VMEM((1, LANES), f32),
+                pltpu.VMEM((groups * site_devices // SIDES, 1, LANES), f32),
                 pltpu.VMEM((groups * site_devices, 1, LANES), f32),
                 pltpu.SemaphoreType.DMA((5,)),
                 pltpu.SemaphoreType.DMA((folds,)),
+                pltpu.SemaphoreType.DMA,
+                pltpu.SemaphoreType.DMA((SIDES,)),
+                pltpu.SemaphoreType.DMA,
+                pltpu.SemaphoreType.DMA((SIDES,)),
                 pltpu.SemaphoreType.DMA,
                 pltpu.SemaphoreType.DMA,
                 pltpu.SemaphoreType.DMA,

time: 19.6 us -> 18.9 us (0.964)
  Pallas kernels: 18.9 us -> 18.1 us
    pallas_call x1, Pallas kernels: 18.3 us -> 17.5 us  [per_device(): pl.pallas_call(functools.partial(kernel, groups, site_devices), out_shape...]
where the time goes in v4:
time: 18.9 us; the launch traced here: 18.7 us
  Pallas kernels  18.1 us (96%)
  between operations  0.64 us (3%)
    pallas_call x1, Pallas kernels, per_device(): pl.pallas_call(functools.partial(kernel, groups, site_devices), out_shape...  17.5 us
    pallas_call x1, Pallas kernels, per_device(): pl.pallas_call(finish, out_shape=(jax.ShapeDtypeStruct((1, quarter), f32)...  0.57 us

profile of v4, /device:TPU:0, one launch (start us, length us, event | category | flops | bytes accessed | tf_op | source)
XLA Modules:
  0.0 18.7 jit_solution(3127103946916103417)
XLA Ops:
  0.6 17.5 %shard_map.85.result = f32[4,128]{1,0:T(4,128)S(1)} custom-call(s32[32,8,1024]{2,1,0:T(8,128)} %bitcast.6, s32[8,128]{1,0:T(8,128)} %bitcast.8, s32[2,1023]{1,0:T(2,128)} %bitcast.7, f32[4,2046]{1,0:T(4,128)} %lengths_hbm.1, f32[4,4]{1,0:T(4,128)} %freq_hbm.1, f32[1,4]{1,0:T(1,128)} %bitcast.9), custom_call_target="tpu_custom_call" | custom-call | tf_op jit(solution)/shard_map/pallas_call | solution.py:533
  18.2 0.6 %shard_map.86 = (f32[1,256]{1,0:T(1,128)}, f32[1,1]{1,0:T(1,128)}, f32[1,1]{1,0:T(1,128)}) custom-call(f32[4,128]{1,0:T(4,128)S(1)} %shard_map.85.result), custom_call_target="tpu_custom_call" | custom-call | tf_op jit(solution)/shard_map/pallas_call | solution.py:593
